TPU v7x, 32 devices: a whole 2x2x4 slice. The times are simulated.
32 devices in a mesh: row: 16 (over z, y, core), rows: 2 (over x).
Axes of the slice: x: 2, y: 2, z: 4, core: 2. Of those that a mesh axis runs over, the one named last changes fastest.
Arguments:
- hopping: float32 [2, 128, 512, 512], P(None, 'row', 'rows'), may hold values from -0.5 to 0.5
- lattice: int32 [3, 128], replicated, may hold values from -4 to 4
- kgrid: int32 [3, 32], replicated, may hold values from 0 to 7
- tangent: float32 [3, 32], replicated, may hold values from -4 to 4
- states: float32 [2, 32, 1024, 512], P(None, 'row'), may hold values from -6 to 6
Outputs:
- energies: float32 [32, 1024], P('row')
- velocities: float32 [32, 1024], P('row')
All inputs are finite; a program needn't handle non-finite values.
Results may differ from a plain program's by a relative error of at most 0.000075.
Values sent between devices are 32-bit elements; how exact they have to be, the bound alone decides.
A program may use at most 256 MiB of HBM per device.

v0:
```python
import math

import jax
import jax.numpy as jnp
from jax import lax
from jax.sharding import PartitionSpec as P

KGRID = 8


def phases(kgrid, lattice, tangent):
    turns = jnp.mod(jnp.sum(kgrid[:, :, None] * lattice[:, None, :], axis=0), KGRID)
    angle = turns.astype(jnp.float32) * (2.0 * math.pi / KGRID)
    weight = jnp.sum(tangent[:, :, None] * lattice[:, None, :].astype(jnp.float32), axis=0)
    return (jnp.cos(angle), jnp.sin(angle), weight)


def expand(first, second, hopping):
    real_sum = jnp.einsum("kr,rab->kab", first, hopping[0], precision=lax.Precision.HIGHEST)
    imag_sum = jnp.einsum("kr,rab->kab", second, hopping[1], precision=lax.Precision.HIGHEST)
    cross_one = jnp.einsum("kr,rab->kab", second, hopping[0], precision=lax.Precision.HIGHEST)
    cross_two = jnp.einsum("kr,rab->kab", first, hopping[1], precision=lax.Precision.HIGHEST)
    return (real_sum - imag_sum, cross_one + cross_two)


def project(m_re, m_im, rows, cols):
    high = lax.Precision.HIGHEST
    y_re = jnp.einsum("kac,kic->kai", m_re, cols[0], precision=high) - jnp.einsum(
        "kac,kic->kai", m_im, cols[1], precision=high
    )
    y_im = jnp.einsum("kac,kic->kai", m_re, cols[1], precision=high) + jnp.einsum(
        "kac,kic->kai", m_im, cols[0], precision=high
    )
    return jnp.einsum("kia,kai->ki", rows[0], y_re, precision=high) + jnp.einsum(
        "kia,kai->ki", rows[1], y_im, precision=high
    )


def per_device(hopping, lattice, kgrid, tangent, states):
    local_r = hopping.shape[1]
    row_count = hopping.shape[2]
    row_start = lax.axis_index("rows") * row_count
    state_rows = lax.dynamic_slice_in_dim(states, row_start, row_count, 3)
    first_r = lax.axis_index("row") * local_r
    mine = lax.dynamic_slice_in_dim(lattice, first_r, local_r, 1)
    cosine, sine, weight = phases(kgrid, mine, tangent)
    hk_re, hk_im = expand(cosine, sine, hopping)
    dk_re, dk_im = expand(-weight * sine, weight * cosine, hopping)
    tiles = lax.psum_scatter(
        jnp.stack([hk_re, hk_im, dk_re, dk_im], axis=1), "row", scatter_dimension=0, tiled=True
    )
    p_h = project(tiles[:, 0], tiles[:, 1], state_rows, states)
    p_d = project(tiles[:, 2], tiles[:, 3], state_rows, states)
    pieces = jnp.stack([p_h, p_d], axis=1)
    totals = lax.psum(pieces, "rows")
    norm = jnp.sum(states[0] * states[0] + states[1] * states[1], axis=-1)
    return (totals[:, 0] / norm, totals[:, 1] / norm)


def solution(mesh):
    placed = (P(None, "row", "rows", None), P(), P(), P(), P(None, "row", None, None))
    return jax.shard_map(
        per_device,
        mesh=mesh,
        in_specs=placed,
        out_specs=(P("row", None), P("row", None)),
        check_vma=False,
    )
```

profile of v0, /device:TPU:16, one launch (start us, length us, event | category | flops | bytes accessed | tf_op | source)
XLA Modules:
  0.0 947.1 jit_solution(17491481738378193474)
XLA Ops:
  7.2 8.0 fusion.64
  15.5 18.6 %fusion.19 = f32[32,256,512]{2,0,1:T(8,128)} fusion(f32[1,8,256,512]{3,2,1,0:T(8,128)} %get-tuple-element.7, f32[32,8]{0,1:T(8,128)S(1)} %multiply_reduce_fusion.4, s32[32,8]{0,1:T(8,128)S(1)} %multiply_reduce_fusion.5), kind=kOutput, calls=%fused_computation.28 | convolution fusion | flops 402657024 | bytes 20973568 | tf_op jit(solution)/shard_map/kr,rab->kab/dot_general | solution.py:19
  34.1 16.9 %fusion.18 = f32[32,256,512]{2,0,1:T(8,128)} fusion(f32[1,8,256,512]{3,2,1,0:T(8,128)S(1)} %copy-done, f32[32,8]{0,1:T(8,128)S(1)} %multiply_reduce_fusion.4, s32[32,8]{0,1:T(8,128)S(1)} %multiply_reduce_fusion.5), kind=kOutput, calls=%fused_computation.27 | convolution fusion | flops 402656768 | bytes 20973568 | tf_op jit(solution)/shard_map/kr,rab->kab/dot_general | solution.py:21
  51.0 15.0 %fusion.20 = f32[32,256,512]{2,0,1:T(8,128)S(1)} fusion(f32[1,8,256,512]{3,2,1,0:T(8,128)S(1)} %copy-done, s32[32,8]{0,1:T(8,128)S(1)} %multiply_reduce_fusion.5), kind=kOutput, calls=%fused_computation.29 | convolution fusion | flops 402656512 | bytes 20972544 | tf_op jit(solution)/shard_map/kr,rab->kab/dot_general | solution.py:21
  66.0 15.0 %fusion.21 = f32[32,256,512]{2,0,1:T(8,128)S(1)} fusion(f32[1,8,256,512]{3,2,1,0:T(8,128)S(1)} %copy-done, s32[32,8]{0,1:T(8,128)S(1)} %multiply_reduce_fusion.5), kind=kOutput, calls=%fused_computation.30 | convolution fusion | flops 402656512 | bytes 20972544 | tf_op jit(solution)/shard_map/kr,rab->kab/dot_general | solution.py:19
  81.0 20.1 %subtract_bitcast_fusion = f32[32,1,256,512]{3,0,2,1:T(8,128)} fusion(f32[32,256,512]{2,0,1:T(8,128)} %fusion.19, f32[1,8,256,512]{3,2,1,0:T(8,128)} %get-tuple-element.6, f32[32,8]{0,1:T(8,128)S(1)} %multiply_reduce_fusion.4, s32[32,8]{0,1:T(8,128)S(1)} %multiply_reduce_fusion.5), kind=kOutput, calls=%fused_computation.2 | convolution fusion | flops 406851072 | bytes 37750784 | tf_op jit(solution)/shard_map/kr,rab->kab/dot_general | solution.py:20
  101.1 20.5 %add_bitcast_fusion = f32[32,1,256,512]{3,0,2,1:T(8,128)} fusion(f32[32,256,512]{2,0,1:T(8,128)} %fusion.18, f32[1,8,256,512]{3,2,1,0:T(8,128)} %get-tuple-element.6, f32[32,8]{0,1:T(8,128)S(1)} %multiply_reduce_fusion.4, s32[32,8]{0,1:T(8,128)S(1)} %multiply_reduce_fusion.5), kind=kOutput, calls=%fused_computation.1 | convolution fusion | flops 406851328 | bytes 37750784 | tf_op jit(solution)/shard_map/kr,rab->kab/dot_general | solution.py:22
  121.5 19.5 %add_bitcast_fusion.1 = f32[32,1,256,512]{3,0,2,1:T(8,128)} fusion(f32[32,256,512]{2,0,1:T(8,128)S(1)} %fusion.20, f32[1,8,256,512]{3,2,1,0:T(8,128)} %get-tuple-element.6, s32[32,8]{0,1:T(8,128)S(1)} %multiply_reduce_fusion.5), kind=kOutput, calls=%fused_computation.3 | convolution fusion | flops 406850816 | bytes 37749760 | tf_op jit(solution)/shard_map/kr,rab->kab/dot_general | solution.py:22
  141.0 19.5 %subtract_bitcast_fusion.1 = f32[32,1,256,512]{3,0,2,1:T(8,128)} fusion(f32[32,256,512]{2,0,1:T(8,128)S(1)} %fusion.21, f32[1,8,256,512]{3,2,1,0:T(8,128)} %get-tuple-element.6, s32[32,8]{0,1:T(8,128)S(1)} %multiply_reduce_fusion.5), kind=kOutput, calls=%fused_computation.4 | convolution fusion | flops 406850816 | bytes 37749760 | tf_op jit(solution)/shard_map/kr,rab->kab/dot_general | solution.py:20
  160.5 43.8 %pad_maximum_fusion = f32[32,4,256,512]{3,0,2,1:T(8,128)} fusion(f32[32,1,256,512]{3,0,2,1:T(8,128)} %add_bitcast_fusion, f32[32,1,256,512]{3,0,2,1:T(8,128)} %subtract_bitcast_fusion, f32[32,1,256,512]{3,0,2,1:T(8,128)} %add_bitcast_fusion.1, f32[32,1,256,512]{3,0,2,1:T(8,128)} %subtract_bitcast_fusion.1), kind=kLoop, calls=%fused_computation | loop fusion | flops 50331648 | bytes 134217728 | tf_op jit(solution)/shard_map/stack | solution.py:50
  204.3 56.4 %copy.14 = f32[32,4,256,512]{3,2,1,0:T(8,128)} copy(f32[32,4,256,512]{3,0,2,1:T(8,128)} %pad_maximum_fusion) | data formatting | bytes 134217728 | tf_op jit(solution)/shard_map/stack | solution.py:50
  260.7 4.0 dynamic-slice_bitcast_fusion
  266.6 2.3 copy.23
  268.9 5.6 fusion.9
  274.5 619.1 %reduce-scatter.2.cloned.1.call-done = f32[2,4,256,512]{3,2,1,0:T(8,128)} async-done(((f32[32,4,256,512]{3,2,1,0:T(8,128)}), f32[2,4,256,512]{3,2,1,0:T(8,128)}) %reduce-scatter.2.cloned.1.call-update) | async-done | bytes 4194320 | tf_op jit(solution)/shard_map/reduce_scatter | solution.py:49
  893.6 6.3 fusion.4
  899.9 6.3 fusion.6
  906.2 5.7 fusion
  912.0 3.7 fusion.2
  915.7 3.8 multiply_reduce_fusion.2
  919.4 3.8 multiply_reduce_fusion
  923.2 4.0 multiply_reduce_fusion.3
  927.3 3.8 multiply_reduce_fusion.1
  931.1 8.1 psum.7
  (26 shorter events, 2.8 us)
Async XLA Ops:
  7.2 886.5 %reduce-scatter.2.cloned.1.call-start = ((), (), s32[]{:S(2)}) async-start(), calls=%async_computation.1 | async-start | bytes 71303168 | tf_op jit(solution)/shard_map/reduce_scatter | solution.py:49
  7.2 8.1 copy-start.3
  7.2 8.1 copy-start.4
  7.2 8.2 copy-start.5
  15.5 18.6 %copy-start = (f32[1,8,256,512]{3,2,1,0:T(8,128)S(1)}, f32[1,8,256,512]{3,2,1,0:T(8,128)}, u32[]{:S(2)}) copy-start(f32[1,8,256,512]{3,2,1,0:T(8,128)} %get-tuple-element.7) | copy-start | bytes 12582916
  893.6 12.6 %copy-start.2 = (f32[2,4,256,512]{3,2,1,0:T(8,128)S(1)}, f32[2,4,256,512]{3,2,1,0:T(8,128)}, u32[]{:S(2)}) copy-start(f32[2,4,256,512]{3,2,1,0:T(8,128)} %reduce-scatter.2.cloned.1.call-done) | copy-start | bytes 12582916
  893.6 18.3 %slice-start = ((s8[8388608]{0:T(1024)(128)(4,1)}), s8[4194304]{0:T(1024)(128)(4,1)S(1)}, s32[]{:S(2)}) async-start(s8[8388608]{0:T(1024)(128)(4,1)} %bitcast.122), calls=%async_computation.2 | async-start | bytes 8388608
  899.9 12.0 %slice-start.1 = ((s8[8388608]{0:T(1024)(128)(4,1)}), s8[4194304]{0:T(1024)(128)(4,1)S(1)}, s32[]{:S(2)}) async-start(s8[8388608]{0:T(1024)(128)(4,1)} %bitcast.122), calls=%async_computation.3 | async-start | bytes 8388608
  911.9 3.7 copy-start.1
Sparse Core Ops, SparseCore 0:
  260.9 632.7 reduce-scatter.1
where the time goes:
time: 956 us; the launch traced here: 947 us
  waiting for transfers between devices  619 us (65%)
  matrix products  182 us (19%)
  local copies, waits for them, and re-layouts  72.7 us (8%)
  other arithmetic  50.3 us (5%)
  between operations  14.7 us (2%)
    reduce_scatter x1, waiting for transfers between devices, per_device(): lax.psum_scatter(jnp.stack([hk_re, hk_im, dk_re, dk_im], axis=1), 'row',...  619 us
    another operation x1, local copies, waits for them, and re-layouts, per_device(): jnp.stack([hk_re, hk_im, dk_re, dk_im], axis=1)  56.4 us
    another operation x1, other arithmetic, per_device(): jnp.stack([hk_re, hk_im, dk_re, dk_im], axis=1)  43.8 us
    dot_general x2, matrix products, expand(): jnp.einsum('kr,rab->kab', first, hopping[1], precision=lax.Precision.HIGH...  39.9 us
    dot_general x2, matrix products, expand(): jnp.einsum('kr,rab->kab', second, hopping[1], precision=lax.Precision.HIG...  39.6 us
    dot_general x2, matrix products, expand(): jnp.einsum('kr,rab->kab', first, hopping[0], precision=lax.Precision.HIGH...  33.6 us
    dot_general x2, matrix products, expand(): jnp.einsum('kr,rab->kab', second, hopping[0], precision=lax.Precision.HIG...  31.9 us
  transfers between devices with their start and end apart: 1, of which 1 were waited for; matrix products, arithmetic and copies ran while one was open for 1% of the time, Pallas kernels for 0%

commit v1 on v0

v1 whole, which is shorter than its diff:
```python
import math

import jax
import jax.numpy as jnp
from jax import lax
from jax.sharding import PartitionSpec as P

KGRID = 8


def phases(kgrid, lattice, tangent):
    turns = jnp.mod(jnp.sum(kgrid[:, :, None] * lattice[:, None, :], axis=0), KGRID)
    angle = turns.astype(jnp.float32) * (2.0 * math.pi / KGRID)
    weight = jnp.sum(tangent[:, :, None] * lattice[:, None, :].astype(jnp.float32), axis=0)
    return (jnp.cos(angle), jnp.sin(angle), weight)


def project(m_re, m_im, rows, cols):
    high = lax.Precision.HIGH
    y_re = jnp.einsum("kmac,kic->kmai", m_re, cols[0], precision=high) - jnp.einsum(
        "kmac,kic->kmai", m_im, cols[1], precision=high
    )
    y_im = jnp.einsum("kmac,kic->kmai", m_re, cols[1], precision=high) + jnp.einsum(
        "kmac,kic->kmai", m_im, cols[0], precision=high
    )
    a = jnp.swapaxes(rows[0], 1, 2)[:, None]
    b = jnp.swapaxes(rows[1], 1, 2)[:, None]
    return jnp.sum(a * y_re + b * y_im, axis=2)


def per_device(hopping, lattice, kgrid, tangent, states):
    row_count = hopping.shape[2]
    row_start = lax.axis_index("rows") * row_count
    state_rows = lax.dynamic_slice_in_dim(states, row_start, row_count, 3)
    cosine, sine, weight = phases(kgrid, lattice, tangent)
    slab = lax.all_to_all(hopping, "row", 2, 1, tiled=True)
    first_d, second_d = -weight * sine, weight * cosine
    coef = jnp.stack(
        [
            jnp.stack([cosine, -sine], axis=1),
            jnp.stack([sine, cosine], axis=1),
            jnp.stack([first_d, -second_d], axis=1),
            jnp.stack([second_d, first_d], axis=1),
        ],
        axis=1,
    )
    blocks = jnp.einsum("kmpr,prac->kmac", coef, slab, precision=lax.Precision.HIGHEST)
    tiles = lax.all_to_all(blocks, "row", 0, 2, tiled=True)
    m_re = tiles[:, 0::2]
    m_im = tiles[:, 1::2]
    pieces = project(m_re, m_im, state_rows, states)
    totals = lax.psum(pieces, "rows")
    norm = jnp.sum(states[0] * states[0] + states[1] * states[1], axis=-1)
    return (totals[:, 0] / norm, totals[:, 1] / norm)


def solution(mesh):
    placed = (P(None, "row", "rows", None), P(), P(), P(), P(None, "row", None, None))
    return jax.shard_map(
        per_device,
        mesh=mesh,
        in_specs=placed,
        out_specs=(P("row", None), P("row", None)),
        check_vma=False,
    )
```

time: 956 us -> 347 us (0.36)
  waiting for transfers between devices: 619 us -> 261 us
  matrix products: 182 us -> 32.4 us
  other arithmetic: 50.3 us -> 4.96 us
  local copies, waits for them, and re-layouts: 72.7 us -> 28.1 us
  between operations: 14.7 us -> 0.73 us
  starting transfers between devices: 0.04 us -> 11 us
    reduce_scatter x1 -> x0, waiting for transfers between devices: 619 us -> none  [per_device(): lax.psum_scatter(jnp.stack([hk_re, hk_im, dk_re, dk_im], axis=1), 'row',...]
    all_to_all x0 -> x2, waiting for transfers between devices: none -> 261 us  [the longest x1 182 us: per_device(): slab = lax.all_to_all(hopping, 'row', 2, 1, tiled=True)]
    dot_general x16 -> x5, matrix products: 182 us -> 32.4 us  [the longest x1 7.58 us: project(): jnp.einsum('kmac,kic->kmai', m_im, cols[1], precision=high)]
    another operation x1 -> x0, local copies, waits for them, and re-layouts: 56.4 us -> none  [per_device(): jnp.stack([hk_re, hk_im, dk_re, dk_im], axis=1)]
    another operation x3 -> x1, other arithmetic: 43.8 us -> 0.01 us  [per_device(): jnp.stack([jnp.stack([cosine, -sine], axis=1), jnp.stack([sine, cosine],...]
    all_to_all x0 -> x2, starting transfers between devices: none -> 11 us  [the longest x1 6.32 us: per_device(): slab = lax.all_to_all(hopping, 'row', 2, 1, tiled=True)]
  transfers between devices with their start and end apart: 1 -> 2, of which waited for: 1 -> 2; matrix products, arithmetic and copies ran while one was open for 1% -> 4% of each run, Pallas kernels for 0% -> 0%
where the time goes in v1:
time: 347 us
  waiting for transfers between devices  261 us (75%)
  matrix products  32.4 us (9%)
  local copies, waits for them, and re-layouts  28.1 us (8%)
  starting transfers between devices  11 us (3%)
  blocking collectives  8.15 us (2%)
  other arithmetic  4.96 us (1%)
    all_to_all x1, waiting for transfers between devices, per_device(): slab = lax.all_to_all(hopping, 'row', 2, 1, tiled=True)  182 us
    all_to_all x1, waiting for transfers between devices, per_device(): tiles = lax.all_to_all(blocks, 'row', 0, 2, tiled=True)  79.1 us
    unnamed x11, local copies, waits for them, and re-layouts  11.5 us
    psum x1, blocking collectives, per_device(): totals = lax.psum(pieces, 'rows')  8.15 us
    dot_general x1, matrix products, project(): jnp.einsum('kmac,kic->kmai', m_im, cols[1], precision=high)  7.58 us
    dot_general x1, matrix products, project(): jnp.einsum('kmac,kic->kmai', m_re, cols[1], precision=high)  7.48 us
    dot_general x1, matrix products, per_device(): jnp.einsum('kmpr,prac->kmac', coef, slab, precision=lax.Precision.HIGHEST)  6.98 us
  transfers between devices with their start and end apart: 2, of which 2 were waited for; matrix products, arithmetic and copies ran while one was open for 4% of the time, Pallas kernels for 0%

profile of v1, /device:TPU:16, one launch (start us, length us, event | category | flops | bytes accessed | tf_op | source)
XLA Modules:
  0.0 346.6 jit_solution(13309918197815795740)
XLA Ops:
  0.6 11.5 %copy.19 = f32[2,8,256,512]{3,1,0,2:T(8,128)} copy(f32[2,8,256,512]{3,2,1,0:T(8,128)} %param.5) | data formatting | bytes 16777216 | tf_op args[0]
  12.1 6.3 %all-to-all-start = ((f32[2,8,256,512]{3,1,0,2:T(8,128)}), f32[2,8,256,512]{3,1,0,2:T(8,128)}, u32[]{:S(2)}, u32[]{:S(2)}) async-start(f32[2,8,256,512]{3,1,0,2:T(8,128)} %copy.19), calls=%async_computation | async-start | bytes 16777216 | tf_op jit(solution)/shard_map/all_to_all | solution.py:36
  18.4 0.0 copy-done.1
  18.4 0.1 multiply_reduce_fusion.1
  18.5 0.0 copy-done.2
  18.5 0.1 multiply_reduce_fusion
  18.6 0.1 fusion.41
  18.7 182.2 %all-to-all-done = f32[2,8,256,512]{3,1,0,2:T(8,128)} async-done(((f32[2,8,256,512]{3,1,0,2:T(8,128)}), f32[2,8,256,512]{3,1,0,2:T(8,128)}, u32[]{:S(2)}, u32[]{:S(2)}) %all-to-all-start) | async-done | bytes 8388640 | tf_op jit(solution)/shard_map/all_to_all | solution.py:36
  200.9 7.0 %fusion.17 = f32[32,4,16,512]{3,0,2,1:T(8,128)S(1)} fusion(f32[2,8,16,16,512]{4,1,0,3,2:T(8,128)} %bitcast.10, f32[32,1,2,128]{3,0,2,1:T(8,128)S(1)} %get-tuple-element.18, f32[32,1,2,128]{3,0,2,1:T(8,128)S(1)} %get-tuple-element.19, f32[32,1,2,128]{3,0,2,1:T(8,128)S(1)} %get-tuple-element.10, f32[32,1,2,128]{3,0,2,1:T(8,128)S(1)} %get-tuple-element.9), kind=kOutput, calls=%fused_computation.20 | convolution fusion | flops 3221323776 | bytes 12713984 | tf_op jit(solution)/shard_map/kmpr,prac->kmac/dot_general | solution.py:47
  207.9 4.4 %copy.21 = f32[32,4,16,512]{3,2,1,0:T(8,128)} copy(f32[32,4,16,512]{3,0,2,1:T(8,128)S(1)} %fusion.17) | data formatting | bytes 8388608 | tf_op jit(solution)/shard_map/kmpr,prac->kmac/dot_general | solution.py:47
  212.3 4.7 %all-to-all-start.1 = ((f32[32,4,16,512]{3,2,1,0:T(8,128)}), f32[32,4,16,512]{3,2,1,0:T(8,128)}, u32[]{:S(2)}, u32[]{:S(2)}) async-start(f32[32,4,16,512]{3,2,1,0:T(8,128)} %copy.21), calls=%async_computation.1 | async-start | bytes 8388608 | tf_op jit(solution)/shard_map/all_to_all | solution.py:48
  217.0 4.6 %dynamic-slice_bitcast_fusion.1 = (f32[2,256,1024]{1,2,0:T(8,128)}, f32[2,256,1024]{1,2,0:T(8,128)}) fusion(f32[2,2,1024,512]{3,2,1,0:T(8,128)} %param.9, s32[]{:T(128)S(6)} %select_n.37, s32[]{:T(128)S(6)} %add.52), kind=kLoop, calls=%fused_computation.22 | loop fusion | bytes 8388616 | tf_op jit(solution)/shard_map/transpose | solution.py:26
  221.6 1.9 copy.18
  223.5 2.9 copy.23
  226.4 4.1 %fusion.12 = f32[2,1024]{1,0:T(2,128)S(1)} fusion(f32[2,2,1024,512]{3,2,1,0:T(8,128)} %param.9), kind=kLoop, calls=%fused_computation.13 | loop fusion | flops 4192256 | bytes 8396800 | tf_op jit(solution)/shard_map/reduce_sum | solution.py:53
  230.5 79.1 %all-to-all-done.1 = f32[32,4,16,512]{3,2,1,0:T(8,128)} async-done(((f32[32,4,16,512]{3,2,1,0:T(8,128)}), f32[32,4,16,512]{3,2,1,0:T(8,128)}, u32[]{:S(2)}, u32[]{:S(2)}) %all-to-all-start.1) | async-done | bytes 4194336 | tf_op jit(solution)/shard_map/all_to_all | solution.py:48
  309.6 2.8 copy.22
  312.4 0.0 slice-start.1
  312.4 7.5 %fusion.7 = f32[2,2,256,1024]{3,2,1,0:T(8,128)} fusion(f32[2,2,1024,512]{3,2,1,0:T(8,128)} %param.9, f32[2,4,256,512]{3,2,1,0:T(8,128)S(1)} %bitcast.93), kind=kOutput, calls=%fused_computation.7 | convolution fusion | flops 3221225472 | bytes 10485760 | tf_op jit(solution)/shard_map/kmac,kic->kmai/dot_general | solution.py:23
  319.9 5.2 %fusion.3 = f32[2,2,256,1024]{3,2,1,0:T(8,128)} fusion(f32[2,2,1024,512]{3,2,1,0:T(8,128)S(1)} %bitcast.92, f32[2,4,256,512]{3,2,1,0:T(8,128)S(1)} %bitcast.94), kind=kOutput, calls=%fused_computation.3 | convolution fusion | flops 3221225472 | bytes 10485760 | tf_op jit(solution)/shard_map/kmac,kic->kmai/dot_general | solution.py:23
  325.1 5.1 %fusion.5 = f32[2,2,256,1024]{3,2,1,0:T(8,128)} fusion(f32[2,2,1024,512]{3,2,1,0:T(8,128)S(1)} %bitcast.92, f32[2,4,256,512]{3,2,1,0:T(8,128)S(1)} %bitcast.95), kind=kOutput, calls=%fused_computation.5 | convolution fusion | flops 3221225472 | bytes 10485760 | tf_op jit(solution)/shard_map/kmac,kic->kmai/dot_general | solution.py:20
  330.2 7.6 %add_reduce_fusion = f32[2,2,1024]{2,1,0:T(2,128)S(1)} fusion(f32[2,2,256,1024]{3,2,1,0:T(8,128)} %fusion.7, f32[2,2,256,1024]{3,2,1,0:T(8,128)} %fusion.3, f32[2,2,256,1024]{3,2,1,0:T(8,128)} %fusion.5, f32[2,2,1024,512]{3,2,1,0:T(8,128)S(1)} %bitcast.92, f32[2,256,1024]{2,1,0:T(8,128)} %copy.23, f32[2,256,1024]{2,1,0:T(8,128)S(1)} %copy.18, ...), kind=kOutput, calls=%fused_computation.15 | convolution fusion | flops 3227512832 | bytes 23085056 | tf_op jit(solution)/shard_map/kmac,kic->kmai/dot_general | solution.py:20
  337.8 8.2 %psum.7 = f32[2,2,1024]{2,1,0:T(2,128)S(1)} all-reduce(f32[2,2,1024]{2,1,0:T(2,128)S(1)} %add_reduce_fusion), channel_id=1, replica_groups=mesh['row'=16,'rows'=2] {'rows'}, use_global_device_ids=true, to_apply=%region_3.4 | all-reduce | flops 4096 | bytes 32768 | tf_op jit(solution)/shard_map/psum | solution.py:52
  346.0 0.6 bitcast_divide_fusion
  (11 shorter events, 0.0 us)
Async XLA Ops:
  12.1 6.3 %copy-start = (s32[3,128]{1,0:T(4,128)S(1)}, s32[3,128]{1,0:T(4,128)}, u32[]{:S(2)}) copy-start(s32[3,128]{1,0:T(4,128)} %param.6) | copy-start | bytes 4612
  12.1 6.3 %copy-start.1 = (s32[3,32]{1,0:T(4,128)S(1)}, s32[3,32]{1,0:T(4,128)}, u32[]{:S(2)}) copy-start(s32[3,32]{1,0:T(4,128)} %param.7) | copy-start | bytes 1156
  12.1 6.4 %copy-start.2 = (f32[3,32]{1,0:T(4,128)S(1)}, f32[3,32]{1,0:T(4,128)}, u32[]{:S(2)}) copy-start(f32[3,32]{1,0:T(4,128)} %param.8) | copy-start | bytes 1156
  12.1 188.9 %all-to-all-start = ((f32[2,8,256,512]{3,1,0,2:T(8,128)}), f32[2,8,256,512]{3,1,0,2:T(8,128)}, u32[]{:S(2)}, u32[]{:S(2)}) async-start(f32[2,8,256,512]{3,1,0,2:T(8,128)} %copy.19), calls=%async_computation | async-start | bytes 16777216 | tf_op jit(solution)/shard_map/all_to_all | solution.py:36
  212.3 97.2 %all-to-all-start.1 = ((f32[32,4,16,512]{3,2,1,0:T(8,128)}), f32[32,4,16,512]{3,2,1,0:T(8,128)}, u32[]{:S(2)}, u32[]{:S(2)}) async-start(f32[32,4,16,512]{3,2,1,0:T(8,128)} %copy.21), calls=%async_computation.1 | async-start | bytes 8388608 | tf_op jit(solution)/shard_map/all_to_all | solution.py:48
  309.6 10.3 %slice-start = ((s8[8388608]{0:T(1024)(128)(4,1)}), s8[4194304]{0:T(1024)(128)(4,1)S(1)}, s32[]{:S(2)}) async-start(s8[8388608]{0:T(1024)(128)(4,1)} %bitcast.91), calls=%async_computation.2 | async-start | bytes 8388608
  312.4 7.5 %slice-start.1 = ((s8[8388608]{0:T(1024)(128)(4,1)}), s8[4194304]{0:T(1024)(128)(4,1)S(1)}, s32[]{:S(2)}) async-start(s8[8388608]{0:T(1024)(128)(4,1)} %bitcast.91), calls=%async_computation.3 | async-start | bytes 8388608

commit v2 on v1

--- a/solution.py
+++ b/solution.py
@@ -33,7 +33,6 @@
     row_start = lax.axis_index("rows") * row_count
     state_rows = lax.dynamic_slice_in_dim(states, row_start, row_count, 3)
     cosine, sine, weight = phases(kgrid, lattice, tangent)
-    slab = lax.all_to_all(hopping, "row", 2, 1, tiled=True)
     first_d, second_d = -weight * sine, weight * cosine
     coef = jnp.stack(
         [
@@ -44,11 +43,20 @@
         ],
         axis=1,
     )
-    blocks = jnp.einsum("kmpr,prac->kmac", coef, slab, precision=lax.Precision.HIGHEST)
-    tiles = lax.all_to_all(blocks, "row", 0, 2, tiled=True)
-    m_re = tiles[:, 0::2]
-    m_im = tiles[:, 1::2]
-    pieces = project(m_re, m_im, state_rows, states)
+    halves = 2 if row_count % (2 * lax.axis_size("row")) == 0 else 1
+    part = row_count // halves
+    slabs = [
+        lax.all_to_all(hopping[:, :, h * part : (h + 1) * part], "row", 2, 1, tiled=True)
+        for h in range(halves)
+    ]
+    tiles = []
+    for slab in slabs:
+        blocks = jnp.einsum("kmpr,prac->kmac", coef, slab, precision=lax.Precision.HIGHEST)
+        tiles.append(lax.all_to_all(blocks, "row", 0, 2, tiled=True))
+    pieces = 0.0
+    for h, tile in enumerate(tiles):
+        rows = state_rows[..., h * part : (h + 1) * part]
+        pieces = pieces + project(tile[:, 0::2], tile[:, 1::2], rows, states)
     totals = lax.psum(pieces, "rows")
     norm = jnp.sum(states[0] * states[0] + states[1] * states[1], axis=-1)
     return (totals[:, 0] / norm, totals[:, 1] / norm)

time: 347 us -> 342 us (0.986)
  waiting for transfers between devices: 261 us -> 234 us
  starting transfers between devices: 11 us -> 19.9 us
  local copies, waits for them, and re-layouts: 28.1 us -> 36.1 us
  matrix products: 32.4 us -> 37.1 us
    all_to_all x2 -> x4, waiting for transfers between devices: 261 us -> 234 us  [the longest x2 172 us: per_device(): lax.all_to_all(hopping[:, :, h * part:(h + 1) * part], 'row', 2, 1, tiled...]
    all_to_all x2 -> x4, starting transfers between devices: 11 us -> 19.9 us  [the longest x2 10.8 us: per_device(): lax.all_to_all(hopping[:, :, h * part:(h + 1) * part], 'row', 2, 1, tiled...]
    slice x0 -> x1, local copies, waits for them, and re-layouts: none -> 6.62 us  [per_device(): hopping[:, :, h * part:(h + 1) * part]]
    dot_general x1 -> x2, matrix products: 5.19 us -> 7.88 us  [project(): jnp.einsum('kmac,kic->kmai', m_im, cols[0], precision=high)]
    dot_general x1 -> x2, matrix products: 7.48 us -> 9.83 us  [project(): jnp.einsum('kmac,kic->kmai', m_re, cols[1], precision=high)]
    dot_general x1 -> x2, matrix products: 7.58 us -> 5.45 us  [project(): jnp.einsum('kmac,kic->kmai', m_im, cols[1], precision=high)]
    unnamed x11 -> x32, local copies, waits for them, and re-layouts: 11.5 us -> 13.2 us
    dot_general x1 -> x2, matrix products: 6.98 us -> 8.32 us  [per_device(): jnp.einsum('kmpr,prac->kmac', coef, slab, precision=lax.Precision.HIGHEST)]
  transfers between devices with their start and end apart: 2 -> 4, of which waited for: 2 -> 4; matrix products, arithmetic and copies ran while one was open for 4% -> 14% of each run, Pallas kernels for 0% -> 0%
where the time goes in v2:
time: 342 us
  waiting for transfers between devices  234 us (68%)
  matrix products  37.1 us (11%)
  local copies, waits for them, and re-layouts  36.1 us (11%)
  starting transfers between devices  19.9 us (6%)
  blocking collectives  8.15 us (2%)
  other arithmetic  5.11 us (1%)
    all_to_all x2, waiting for transfers between devices, per_device(): lax.all_to_all(hopping[:, :, h * part:(h + 1) * part], 'row', 2, 1, tiled...  172 us
    all_to_all x2, waiting for transfers between devices, per_device(): tiles.append(lax.all_to_all(blocks, 'row', 0, 2, tiled=True))  62.5 us
    unnamed x32, local copies, waits for them, and re-layouts  13.2 us
    all_to_all x2, starting transfers between devices, per_device(): lax.all_to_all(hopping[:, :, h * part:(h + 1) * part], 'row', 2, 1, tiled...  10.8 us
    dot_general x2, matrix products, project(): jnp.einsum('kmac,kic->kmai', m_re, cols[1], precision=high)  9.83 us
    all_to_all x2, starting transfers between devices, per_device(): tiles.append(lax.all_to_all(blocks, 'row', 0, 2, tiled=True))  9.17 us
    dot_general x2, matrix products, per_device(): jnp.einsum('kmpr,prac->kmac', coef, slab, precision=lax.Precision.HIGHEST)  8.32 us
    psum x1, blocking collectives, per_device(): totals = lax.psum(pieces, 'rows')  8.15 us
  transfers between devices with their start and end apart: 4, of which 4 were waited for; matrix products, arithmetic and copies ran while one was open for 14% of the time, Pallas kernels for 0%

profile of v2, /device:TPU:16, one launch (start us, length us, event | category | flops | bytes accessed | tf_op | source)
XLA Modules:
  0.0 341.6 jit_solution(9086962714207219015)
XLA Ops:
  0.6 6.6 %fusion.61 = (f32[2,8,128,512]{3,2,1,0:T(8,128)S(1)}, f32[2,8,128,512]{3,2,1,0:T(8,128)}) fusion(f32[2,8,256,512]{3,2,1,0:T(8,128)} %param.5), kind=kLoop, calls=%fused_computation.77 | loop fusion | bytes 16777216 | tf_op jit(solution)/shard_map/slice | solution.py:49
  7.2 4.4 %copy.48 = f32[2,8,128,512]{3,1,0,2:T(8,128)} copy(f32[2,8,128,512]{3,2,1,0:T(8,128)S(1)} %get-tuple-element.8) | data formatting | bytes 8388608
  11.6 6.2 %all-to-all-start.2 = ((f32[2,8,128,512]{3,1,0,2:T(8,128)}), f32[2,8,128,512]{3,1,0,2:T(8,128)}, u32[]{:S(2)}, u32[]{:S(2)}) async-start(f32[2,8,128,512]{3,1,0,2:T(8,128)} %copy.48), calls=%async_computation.2 | async-start | bytes 8388608 | tf_op jit(solution)/shard_map/all_to_all | solution.py:49
  17.8 6.6 %copy.47 = f32[2,8,128,512]{3,1,0,2:T(8,128)} copy(f32[2,8,128,512]{3,2,1,0:T(8,128)} %get-tuple-element.9) | data formatting | bytes 8388608
  24.4 86.1 %all-to-all-done.2 = f32[2,8,128,512]{3,1,0,2:T(8,128)} async-done(((f32[2,8,128,512]{3,1,0,2:T(8,128)}), f32[2,8,128,512]{3,1,0,2:T(8,128)}, u32[]{:S(2)}, u32[]{:S(2)}) %all-to-all-start.2) | async-done | bytes 4194336 | tf_op jit(solution)/shard_map/all_to_all | solution.py:49
  110.4 4.6 %all-to-all-start = ((f32[2,8,128,512]{3,1,0,2:T(8,128)}), f32[2,8,128,512]{3,1,0,2:T(8,128)}, u32[]{:S(2)}, u32[]{:S(2)}) async-start(f32[2,8,128,512]{3,1,0,2:T(8,128)} %copy.47), calls=%async_computation | async-start | bytes 8388608 | tf_op jit(solution)/shard_map/all_to_all | solution.py:49
  115.3 4.2 %fusion.35 = f32[32,4,8,512]{3,0,2,1:T(8,128)S(1)} fusion(f32[2,8,16,8,512]{4,1,0,3,2:T(8,128)} %bitcast.33, f32[32,1,2,128]{3,0,2,1:T(8,128)S(1)} %get-tuple-element.22, f32[32,1,2,128]{3,0,2,1:T(8,128)S(1)} %get-tuple-element.23, f32[32,1,2,128]{3,0,2,1:T(8,128)S(1)} %get-tuple-element.14, f32[32,1,2,128]{3,0,2,1:T(8,128)S(1)} %get-tuple-element.13), kind=kOutput, calls=%fused_computation.39 | convolution fusion | flops 1610711040 | bytes 6422528 | tf_op jit(solution)/shard_map/kmpr,prac->kmac/dot_general | solution.py:54
  119.5 2.6 copy.37
  122.1 85.6 %all-to-all-done = f32[2,8,128,512]{3,1,0,2:T(8,128)} async-done(((f32[2,8,128,512]{3,1,0,2:T(8,128)}), f32[2,8,128,512]{3,1,0,2:T(8,128)}, u32[]{:S(2)}, u32[]{:S(2)}) %all-to-all-start) | async-done | bytes 4194336 | tf_op jit(solution)/shard_map/all_to_all | solution.py:49
  207.7 4.6 %all-to-all-start.3 = ((f32[32,4,8,512]{3,2,1,0:T(8,128)}), f32[32,4,8,512]{3,2,1,0:T(8,128)S(1)}, u32[]{:S(2)}, u32[]{:S(2)}) async-start(f32[32,4,8,512]{3,2,1,0:T(8,128)} %copy.37), calls=%async_computation.3 | async-start | bytes 4194304 | tf_op jit(solution)/shard_map/all_to_all | solution.py:55
  212.3 4.2 %fusion.32 = f32[32,4,8,512]{3,0,2,1:T(8,128)S(1)} fusion(f32[2,8,16,8,512]{4,1,0,3,2:T(8,128)} %bitcast.10, f32[32,1,2,128]{3,0,2,1:T(8,128)S(1)} %get-tuple-element.22, f32[32,1,2,128]{3,0,2,1:T(8,128)S(1)} %get-tuple-element.23, f32[32,1,2,128]{3,0,2,1:T(8,128)S(1)} %get-tuple-element.14, f32[32,1,2,128]{3,0,2,1:T(8,128)S(1)} %get-tuple-element.13), kind=kOutput, calls=%fused_computation.38 | convolution fusion | flops 1610711040 | bytes 6422528 | tf_op jit(solution)/shard_map/kmpr,prac->kmac/dot_general | solution.py:54
  219.0 40.9 %all-to-all-done.3 = f32[32,4,8,512]{3,2,1,0:T(8,128)S(1)} async-done(((f32[32,4,8,512]{3,2,1,0:T(8,128)}), f32[32,4,8,512]{3,2,1,0:T(8,128)S(1)}, u32[]{:S(2)}, u32[]{:S(2)}) %all-to-all-start.3) | async-done | bytes 2097184 | tf_op jit(solution)/shard_map/all_to_all | solution.py:55
  261.2 4.6 %all-to-all-start.1 = ((f32[32,4,8,512]{3,2,1,0:T(8,128)}), f32[32,4,8,512]{3,2,1,0:T(8,128)}, u32[]{:S(2)}, u32[]{:S(2)}) async-start(f32[32,4,8,512]{3,2,1,0:T(8,128)} %copy.31), calls=%async_computation.1 | async-start | bytes 4194304 | tf_op jit(solution)/shard_map/all_to_all | solution.py:55
  265.8 3.5 %dynamic-slice_bitcast_fusion.1 = (f32[2,128,1024]{1,2,0:T(8,128)}, f32[2,128,1024]{1,2,0:T(8,128)S(1)}, f32[2,128,1024]{1,2,0:T(8,128)S(1)}, f32[2,128,1024]{1,2,0:T(8,128)S(1)}) fusion(f32[2,2,1024,512]{3,2,1,0:T(8,128)} %param.9, s32[]{:T(128)S(6)} %add.65, s32[]{:T(128)S(6)} %add.64, s32[]{:T(128)S(6)} %select_n.37), kind=kLoop, calls=%fused_computation.41 | loop fusion | bytes 8388620 | tf_op jit(solution)/shard_map/transpose | solution.py:26
  274.9 4.2 %fusion.21 = f32[2,1024]{1,0:T(2,128)S(1)} fusion(f32[2,2,1024,512]{3,2,1,0:T(8,128)} %param.9), kind=kLoop, calls=%fused_computation.22 | loop fusion | flops 4192256 | bytes 8396800 | tf_op jit(solution)/shard_map/reduce_sum | solution.py:61
  279.4 5.6 %fusion.12 = f32[2,2,128,1024]{3,2,1,0:T(8,128)} fusion(f32[2,2,1024,512]{3,2,1,0:T(8,128)} %param.9, f32[2,4,128,512]{3,2,1,0:T(8,128)S(1)} %bitcast.135), kind=kOutput, calls=%fused_computation.12 | convolution fusion | flops 1610612736 | bytes 7340032 | tf_op jit(solution)/shard_map/kmac,kic->kmai/dot_general | solution.py:23
  285.0 3.4 %fusion.4 = f32[2,2,128,1024]{3,2,1,0:T(8,128)} fusion(f32[2,2,1024,512]{3,2,1,0:T(8,128)S(1)} %bitcast.132, f32[2,4,128,512]{3,2,1,0:T(8,128)S(1)} %bitcast.136), kind=kOutput, calls=%fused_computation.4 | convolution fusion | flops 1610612736 | bytes 7340032 | tf_op jit(solution)/shard_map/kmac,kic->kmai/dot_general | solution.py:23
  288.4 3.5 %fusion.6 = f32[2,2,128,1024]{3,2,1,0:T(8,128)} fusion(f32[2,2,1024,512]{3,2,1,0:T(8,128)S(1)} %bitcast.132, f32[2,4,128,512]{3,2,1,0:T(8,128)S(1)} %bitcast.137), kind=kOutput, calls=%fused_computation.6 | convolution fusion | flops 1610612736 | bytes 7340032 | tf_op jit(solution)/shard_map/kmac,kic->kmai/dot_general | solution.py:20
  291.9 21.6 %all-to-all-done.1 = f32[32,4,8,512]{3,2,1,0:T(8,128)} async-done(((f32[32,4,8,512]{3,2,1,0:T(8,128)}), f32[32,4,8,512]{3,2,1,0:T(8,128)}, u32[]{:S(2)}, u32[]{:S(2)}) %all-to-all-start.1) | async-done | bytes 2097184 | tf_op jit(solution)/shard_map/all_to_all | solution.py:55
  315.5 4.3 %fusion.16 = f32[2,2,128,1024]{3,2,1,0:T(8,128)S(1)} fusion(f32[2,2,1024,512]{3,2,1,0:T(8,128)} %param.9, f32[2,4,128,512]{3,2,1,0:T(8,128)S(1)} %bitcast.139), kind=kOutput, calls=%fused_computation.16 | convolution fusion | flops 1610612736 | bytes 7340032 | tf_op jit(solution)/shard_map/kmac,kic->kmai/dot_general | solution.py:23
  319.8 4.4 %fusion.8 = f32[2,2,128,1024]{3,2,1,0:T(8,128)S(1)} fusion(f32[2,2,1024,512]{3,2,1,0:T(8,128)} %param.9, f32[2,4,128,512]{3,2,1,0:T(8,128)S(1)} %bitcast.140), kind=kOutput, calls=%fused_computation.8 | convolution fusion | flops 1610612736 | bytes 7340032 | tf_op jit(solution)/shard_map/kmac,kic->kmai/dot_general | solution.py:23
  327.3 2.7 add_reduce_fusion
  330.1 2.7 add_reduce_fusion.1
  332.8 8.1 %psum.7 = f32[2,2,1024]{2,1,0:T(2,128)S(1)} all-reduce(f32[2,2,1024]{2,1,0:T(2,128)S(1)} %add.62), channel_id=1, replica_groups=mesh['row'=16,'rows'=2] {'rows'}, use_global_device_ids=true, to_apply=%region_4.5 | all-reduce | flops 4096 | bytes 32768 | tf_op jit(solution)/shard_map/psum | solution.py:60
  (48 shorter events, 15.6 us)
Async XLA Ops:
  11.6 98.8 %all-to-all-start.2 = ((f32[2,8,128,512]{3,1,0,2:T(8,128)}), f32[2,8,128,512]{3,1,0,2:T(8,128)}, u32[]{:S(2)}, u32[]{:S(2)}) async-start(f32[2,8,128,512]{3,1,0,2:T(8,128)} %copy.48), calls=%async_computation.2 | async-start | bytes 8388608 | tf_op jit(solution)/shard_map/all_to_all | solution.py:49
  24.4 90.7 %copy-start.8 = (s32[3,128]{1,0:T(4,128)S(1)}, s32[3,128]{1,0:T(4,128)}, u32[]{:S(2)}) copy-start(s32[3,128]{1,0:T(4,128)} %param.6) | copy-start | bytes 4612
  24.4 90.7 %copy-start.9 = (s32[3,32]{1,0:T(4,128)S(1)}, s32[3,32]{1,0:T(4,128)}, u32[]{:S(2)}) copy-start(s32[3,32]{1,0:T(4,128)} %param.7) | copy-start | bytes 1156
  24.4 90.8 %copy-start.10 = (f32[3,32]{1,0:T(4,128)S(1)}, f32[3,32]{1,0:T(4,128)}, u32[]{:S(2)}) copy-start(f32[3,32]{1,0:T(4,128)} %param.8) | copy-start | bytes 1156
  110.4 97.2 %all-to-all-start = ((f32[2,8,128,512]{3,1,0,2:T(8,128)}), f32[2,8,128,512]{3,1,0,2:T(8,128)}, u32[]{:S(2)}, u32[]{:S(2)}) async-start(f32[2,8,128,512]{3,1,0,2:T(8,128)} %copy.47), calls=%async_computation | async-start | bytes 8388608 | tf_op jit(solution)/shard_map/all_to_all | solution.py:49
  207.7 52.2 %all-to-all-start.3 = ((f32[32,4,8,512]{3,2,1,0:T(8,128)}), f32[32,4,8,512]{3,2,1,0:T(8,128)S(1)}, u32[]{:S(2)}, u32[]{:S(2)}) async-start(f32[32,4,8,512]{3,2,1,0:T(8,128)} %copy.37), calls=%async_computation.3 | async-start | bytes 4194304 | tf_op jit(solution)/shard_map/all_to_all | solution.py:55
  259.9 1.3 copy-start
  261.2 52.3 %all-to-all-start.1 = ((f32[32,4,8,512]{3,2,1,0:T(8,128)}), f32[32,4,8,512]{3,2,1,0:T(8,128)}, u32[]{:S(2)}, u32[]{:S(2)}) async-start(f32[32,4,8,512]{3,2,1,0:T(8,128)} %copy.31), calls=%async_computation.1 | async-start | bytes 4194304 | tf_op jit(solution)/shard_map/all_to_all | solution.py:55
  274.9 4.2 %copy-start.1 = (f32[32,4,8,512]{3,2,1,0:T(8,128)S(1)}, f32[32,4,8,512]{3,2,1,0:T(8,128)}, u32[]{:S(2)}) copy-start(f32[32,4,8,512]{3,2,1,0:T(8,128)} %copy-done) | copy-start | bytes 6291460
  274.9 10.0 %slice-start = ((s8[8388608]{0:T(1024)(128)(4,1)}), s8[4194304]{0:T(1024)(128)(4,1)S(1)}, s32[]{:S(2)}) async-start(s8[8388608]{0:T(1024)(128)(4,1)} %bitcast.131), calls=%async_computation.4 | async-start | bytes 8388608
  279.2 5.8 %slice-start.1 = ((s8[8388608]{0:T(1024)(128)(4,1)}), s8[4194304]{0:T(1024)(128)(4,1)S(1)}, s32[]{:S(2)}) async-start(s8[8388608]{0:T(1024)(128)(4,1)} %bitcast.131), calls=%async_computation.5 | async-start | bytes 8388608
  313.5 10.7 %slice-start.2 = ((s8[8388608]{0:T(1024)(128)(4,1)}), s8[4194304]{0:T(1024)(128)(4,1)S(1)}, s32[]{:S(2)}) async-start(s8[8388608]{0:T(1024)(128)(4,1)} %bitcast.133), calls=%async_computation.6 | async-start | bytes 8388608
  315.5 8.8 %slice-start.3 = ((s8[8388608]{0:T(1024)(128)(4,1)}), s8[4194304]{0:T(1024)(128)(4,1)S(1)}, s32[]{:S(2)}) async-start(s8[8388608]{0:T(1024)(128)(4,1)} %bitcast.133), calls=%async_computation.7 | async-start | bytes 8388608
  319.8 6.7 %copy-start.7 = (f32[2,128,1024]{2,1,0:T(8,128)S(1)}, f32[2,128,1024]{2,1,0:T(8,128)}, u32[]{:S(2)}) copy-start(f32[2,128,1024]{2,1,0:T(8,128)} %copy.39) | copy-start | bytes 3145732
  324.2 2.2 copy-start.2
  324.2 2.2 copy-start.3
  324.2 2.8 copy-start.4
  324.3 3.1 copy-start.6
  327.3 2.7 copy-start.5
